TPU v7x, 512 devices: a whole 4x8x8 slice. The times are simulated.
512 devices in a mesh: expert: 32 (over z, y_hi), tensor: 16 (over y_lo, x, core).
Axes of the slice: x: 4, y: 8 (y_hi: 4, y_lo: 2; y = y_hi * 2 + y_lo), z: 8, core: 2. Of those that a mesh axis runs over, the one named last changes fastest.
Arguments:
- tokens: bfloat16 [4096, 3072], P('expert', 'tensor'), may hold values from -6 to 6
- expert_ids: int32 [4096, 2], P('expert'), may hold values from 0 to 7, all different within a row; in each aligned block of 128 rows (0 to 127, 128 to 255, ...) at most 48 rows name the same one
- joined_weight: bfloat16 [32, 3072, 2, 4096], P('expert', 'tensor'), may hold values from -0.109375 to 0.109375
Outputs:
- hidden: bfloat16 [4096, 2, 4, 4096], P('expert', None, None, 'tensor')
Inputs may be any that keep to these rules, and one draw needn't show every extreme that they name: `expert_ids`: each row names 2 different experts. Among the rows of one device (each aligned block of 128 rows) no expert is named by more than 48 rows, and in some blocks one expert is named by exactly 48 rows.
All inputs are finite; a program needn't handle non-finite values.
Results may differ from a plain program's by a relative error of at most 0.001.
Values may be sent and summed in bfloat16 or wider, within the bound.
A program may use at most 128 MiB of HBM per device.

v0:
```python
import jax
import jax.numpy as jnp
from jax import lax
from jax.sharding import PartitionSpec as P

E = 8
TOP = 2
CAP = 48


def activate(gate_up, half_width):
    gate = gate_up[:, :half_width]
    upward = gate_up[:, half_width:]
    return (jax.nn.silu(gate) * upward).astype(jnp.bfloat16)


def give_back(active):
    return lax.all_to_all(active, "expert", split_axis=0, concat_axis=0, tiled=True)


def local(tokens, expert_ids, joined_weight):
    groups = lax.axis_size("tensor")
    blocks = lax.axis_size("expert")
    copies = blocks // E
    local_rows = joined_weight.shape[1]
    half_width = joined_weight.shape[3] // groups
    pieces = joined_weight[0].reshape(local_rows, 2, groups, half_width)
    arranged = lax.all_to_all(pieces, "tensor", split_axis=2, concat_axis=0, tiled=True)
    weights = arranged.reshape(local_rows * groups, 2 * half_width)
    tok_count = tokens.shape[0]
    flat_ids = expert_ids.reshape(-1)
    chosen = (flat_ids[:, None] == jnp.arange(E, dtype=jnp.int32)[None, :]).astype(jnp.int32)
    earlier = jnp.cumsum(chosen, axis=0) - chosen
    position = jnp.sum(earlier * chosen, axis=1)
    slot_index = flat_ids * CAP + position
    pick_table = (slot_index[:, None] == jnp.arange(E * CAP, dtype=jnp.int32)[None, :]).astype(
        jnp.bfloat16
    )
    token_table = pick_table.reshape(tok_count, TOP, E * CAP).sum(axis=1)
    width = tokens.shape[1]
    placed = lax.dot_general(
        token_table, tokens, (((0,), (0,)), ((), ())), preferred_element_type=jnp.float32
    )
    placed = placed.astype(jnp.bfloat16).reshape(E, 1, CAP, width)
    outgoing = jnp.broadcast_to(placed, (E, copies, CAP, width)).reshape(blocks, CAP, width)
    received = lax.all_to_all(outgoing, "expert", split_axis=0, concat_axis=0, tiled=True)
    slot_count = received.shape[1]
    piece = lax.all_gather(received, "tensor", axis=2, tiled=True)
    row_block = piece.reshape(blocks * slot_count, piece.shape[2])
    gate_up = jnp.dot(row_block, weights, preferred_element_type=jnp.float32)
    returned = give_back(activate(gate_up, half_width).reshape(blocks, slot_count, half_width))
    grouped = (
        returned.reshape(E, copies, CAP, half_width)
        .transpose(0, 2, 1, 3)
        .reshape(E * CAP, copies * half_width)
    )
    hidden = jnp.dot(pick_table, grouped, preferred_element_type=jnp.float32).astype(jnp.bfloat16)
    return hidden.reshape(tok_count, TOP, copies, half_width)


def solution(mesh):
    placed = (P("expert", "tensor"), P("expert", None), P("expert", "tensor", None, None))
    return jax.shard_map(
        local,
        mesh=mesh,
        in_specs=placed,
        out_specs=P("expert", None, None, "tensor"),
        check_vma=False,
    )
```

profile of v0, /device:TPU:10, one launch (start us, length us, event | category | flops | bytes accessed | tf_op | source)
XLA Modules:
  0.0 299.9 jit_solution(4116273108823073041)
XLA Ops:
  6.5 0.8 copy.55
  7.5 0.1 eq.46
  7.6 0.6 reduce-window.6
  8.2 0.2 slice_reduce_fusion
  8.6 0.1 reduce_sum.24
  8.8 0.7 multiply_add_fusion
  9.6 0.2 convolution_convert_fusion.1
  9.8 0.1 copy.58
  10.0 37.4 %all_to_all.25 = bf16[32,48,192]{2,1,0:T(8,128)(2,1)S(1)} all-to-all(bf16[32,48,192]{2,1,0:T(8,128)(2,1)S(1)} %bitcast.36), channel_id=1, replica_groups=mesh['expert'=32,'tensor'=16] {'expert'}, dimensions={0} | all-to-all | bytes 1179648 | tf_op jit(solution)/shard_map/all_to_all | solution.py:46
  47.4 2.3 copy.59
  49.7 4.6 %reshape_squeeze.3 = bf16[192,2,16,256]{3,2,1,0:T(8,128)(2,1)S(1)} reshape(bf16[1,192,2,4096]{3,2,1,0:T(2,128)(2,1)} %param.5) | data formatting | bytes 6291456 | tf_op jit(solution)/shard_map/reshape;squeeze | solution.py:27
  54.3 3.0 %copy.61 = bf16[192,2,16,256]{3,1,0,2:T(2,128)(2,1)S(1)} copy(bf16[192,2,16,256]{3,2,1,0:T(8,128)(2,1)S(1)} %reshape_squeeze.3) | data formatting | bytes 6291456 | tf_op jit(solution)/shard_map/reshape;squeeze | solution.py:27
  57.3 75.2 %all_to_all.26 = bf16[192,2,16,256]{3,1,0,2:T(2,128)(2,1)S(1)} all-to-all(bf16[192,2,16,256]{3,1,0,2:T(2,128)(2,1)S(1)} %copy.61), channel_id=1, replica_groups=mesh['expert'=32,'tensor'=16] {'tensor'}, dimensions={2} | all-to-all | bytes 6291456 | tf_op jit(solution)/shard_map/all_to_all | solution.py:28
  132.5 0.5 copy.63
  133.1 86.2 %all-gather.2.cloned.1.call-done = bf16[32,48,3072]{1,0,2:T(8,128)(2,1)} async-done(((bf16[32,48,192]{1,0,2:T(8,128)(2,1)}), bf16[32,48,3072]{1,0,2:T(8,128)(2,1)}) %all-gather.2.cloned.1.call-update) | async-done | bytes 9437200 | tf_op jit(solution)/shard_map/all_gather | solution.py:48
  219.3 26.3 %copy.60 = bf16[32,48,3072]{2,1,0:T(8,128)(2,1)} copy(bf16[32,48,3072]{1,0,2:T(8,128)(2,1)} %all-gather.2.cloned.1.call-done) | data formatting | bytes 18874368 | tf_op jit(solution)/shard_map/all_gather | solution.py:48
  245.5 7.5 %fusion.7 = f32[1536,512]{1,0:T(8,128)S(1)} fusion(bf16[1536,3072]{1,0:T(8,128)(2,1)} %bitcast.31, bf16[3072,512]{1,0:T(8,128)(2,1)S(1)} %bitcast.32), kind=kOutput, calls=%fused_computation.18 | convolution fusion | flops 4831838208 | bytes 15728640 | tf_op jit(solution)/shard_map/dot_general | solution.py:50
  253.1 1.3 fusion
  254.4 9.7 %all-to-all-start.2 = ((bf16[32,48,256]{2,1,0:T(8,128)(2,1)}), bf16[32,48,256]{2,1,0:T(8,128)(2,1)S(1)}, u32[]{:S(2)}, u32[]{:S(2)}) async-start(bf16[32,48,256]{2,1,0:T(8,128)(2,1)} %bitcast.7), calls=%async_computation.2 | async-start | bytes 1572864 | tf_op jit(solution)/shard_map/all_to_all | solution.py:18
  264.1 26.8 %all-to-all-done.2 = bf16[32,48,256]{2,1,0:T(8,128)(2,1)S(1)} async-done(((bf16[32,48,256]{2,1,0:T(8,128)(2,1)}), bf16[32,48,256]{2,1,0:T(8,128)(2,1)S(1)}, u32[]{:S(2)}, u32[]{:S(2)}) %all-to-all-start.2) | async-done | bytes 786464 | tf_op jit(solution)/shard_map/all_to_all | solution.py:18
  290.8 0.4 copy.62
  291.3 0.2 copy.64
  291.4 0.5 convolution_convert_fusion
  291.9 1.2 reshape.70
  (13 shorter events, 0.5 us)
Async XLA Ops:
  6.5 3.1 %copy-start = (bf16[128,192]{0,1:T(8,128)(2,1)S(1)}, bf16[128,192]{0,1:T(8,128)(2,1)}, u32[]{:S(2)}) copy-start(bf16[128,192]{0,1:T(8,128)(2,1)} %param.3) | copy-start | bytes 147460
  6.5 212.7 %all-gather.2.cloned.1.call-start = ((), (), s32[]{:S(2)}) async-start(), calls=%async_computation.3 | async-start | bytes 26738688 | tf_op jit(solution)/shard_map/all_gather | solution.py:48
  254.4 36.5 %all-to-all-start.2 = ((bf16[32,48,256]{2,1,0:T(8,128)(2,1)}), bf16[32,48,256]{2,1,0:T(8,128)(2,1)S(1)}, u32[]{:S(2)}, u32[]{:S(2)}) async-start(bf16[32,48,256]{2,1,0:T(8,128)(2,1)} %bitcast.7), calls=%async_computation.2 | async-start | bytes 1572864 | tf_op jit(solution)/shard_map/all_to_all | solution.py:18
Sparse Core Ops, SparseCore 0:
  49.8 169.3 all-gather.1
where the time goes:
time: 301 us; the launch traced here: 300 us
  blocking collectives  113 us (38%)
  waiting for transfers between devices  113 us (38%)
  local copies, waits for them, and re-layouts  40.1 us (13%)
  between operations  13.5 us (4%)
  starting transfers between devices  9.68 us (3%)
  matrix products  8.2 us (3%)
    all_gather x1, waiting for transfers between devices, local(): piece = lax.all_gather(received, 'tensor', axis=2, tiled=True)  86.2 us
    all_to_all x1, blocking collectives, local(): lax.all_to_all(pieces, 'tensor', split_axis=2, concat_axis=0, tiled=True)  75.2 us
    all_to_all x1, blocking collectives, local(): lax.all_to_all(outgoing, 'expert', split_axis=0, concat_axis=0, tiled=True)  37.4 us
    all_to_all x1, waiting for transfers between devices, give_back(): lax.all_to_all(active, 'expert', split_axis=0, concat_axis=0, tiled=True)  26.8 us
    all_gather x1, local copies, waits for them, and re-layouts, local(): piece = lax.all_gather(received, 'tensor', axis=2, tiled=True)  26.3 us
    all_to_all x1, starting transfers between devices, give_back(): lax.all_to_all(active, 'expert', split_axis=0, concat_axis=0, tiled=True)  9.68 us
    another operation x2, local copies, waits for them, and re-layouts, local(): pieces = joined_weight[0].reshape(local_rows, 2, groups, half_width)  7.59 us
    dot_general x1, matrix products, local(): gate_up = jnp.dot(row_block, weights, preferred_element_type=jnp.float32)  7.53 us
  transfers between devices with their start and end apart: 2, of which 2 were waited for; matrix products, arithmetic and copies ran while one was open for 3% of the time, Pallas kernels for 0%

commit v1 on v0

v1 whole, which is shorter than its diff:
```python
import functools

import jax
import jax.numpy as jnp
from jax import lax
from jax.experimental import pallas as pl
from jax.experimental.pallas import tpu as pltpu
from jax.sharding import PartitionSpec as P

MESH = pl.DeviceIdType.MESH
E = 8
CAP = 48
BF = jnp.bfloat16
F32 = jnp.float32


def kernel(
    tok_ref, ids_ref, idst_ref, w_ref, out_ref,
    xbuf, wrecv, wrelay, wk, tok_own, tok_oth, placed, slots, act, ret,
    ws, wr, rs, rr, fs, own_sem, ts, tr, zs, zr, zl,
    ys, yr, xs, xr, ds, dr, hs, hr, hl,
):
    a, b = lax.axis_index("expert"), lax.axis_index("tensor")
    z, yh = a // 4, a % 4
    yl, x, c = b // 8, (b // 2) % 4, b % 2
    y = 2 * yh + yl

    def dev(zz, yy, xx, cc):
        yy, xx, zz = yy % 8, xx % 4, zz % 8
        return (zz * 4 + yy // 2, (yy % 2) * 8 + xx * 2 + cc)

    yp = y + 1 - 2 * yl
    rows = w_ref.shape[0]
    half = 256

    def remote(src, dst, send, recv, to):
        return pltpu.make_async_remote_copy(
            src_ref=src, dst_ref=dst, send_sem=send, recv_sem=recv,
            device_id=to, device_id_type=MESH,
        )

    me = dev(z, y, x, 1 - c)

    def got(ref, sem):
        remote(ref, ref, sem, sem, me).wait_recv()

    def sent(ref, sem):
        remote(ref, ref, sem, sem, me).wait_send()

    barrier = pltpu.get_barrier_semaphore()
    count = 0

    def greet(to):
        pl.semaphore_signal(barrier, inc=1, device_id=to, device_id_type=MESH)

    for dx in range(4):
        for dy in range(2):
            for dc in range(2):
                if dx or dy or dc:
                    greet(dev(z, y if dy == 0 else yp, x + dx, c if dc == 0 else 1 - c))
                    count += 1
    for k in range(1, 8):
        greet(dev(z + k, y, x, c))
        count += 1
    greet(dev(z, y - 1 + 2 * yl, x, c))
    count += 1

    tok_own[...] = tok_ref[...]
    it = lax.broadcasted_iota
    ids_t = idst_ref[...]
    named = (ids_t[0:1, :] == it(jnp.int32, (8, 128), 0)) | (ids_t[1:2, :] == it(jnp.int32, (8, 128), 0))
    before = (it(jnp.int32, (128, 128), 0) < it(jnp.int32, (128, 128), 1)).astype(F32).astype(BF)
    earlier = jnp.dot(named.astype(F32).astype(BF), before, preferred_element_type=F32)
    slots[...] = jnp.where(named, earlier, -1.0)

    pl.semaphore_wait(barrier, count)

    tok_copy = remote(tok_own, tok_oth, ts, tr, dev(z, y, x, 1 - c))
    tok_copy.start()

    def w_src(px, py, pc):
        col = (py * 8 + px * 2 + pc) * half
        return w_ref.at[:, :, pl.ds(pl.multiple_of(col, half), half)]

    own_w = pltpu.make_async_copy(w_src(x, yl, c), wrecv.at[0, yl, c], own_sem)
    own_w.start()
    other_w = remote(w_src(x, yl, 1 - c), wrecv.at[0, yl, c], ws.at[0], wr.at[0, yl, c], dev(z, y, x, 1 - c))
    other_w.start()

    def w_relay(d, dy):
        pyl = yl if dy == 0 else 1 - yl
        step = 1 if d == 0 else -1
        return remote(
            w_src((x + 2) % 4, pyl, d), wrelay.at[d, dy], rs.at[d, dy], rr.at[d, dy],
            dev(z, y, x + step, c),
        )

    def w_direct(d, dy, pc):
        pyl = yl if dy == 0 else 1 - yl
        step = 1 if d == 0 else -1
        xrel = 3 if d == 0 else 1
        return remote(
            w_src((x + step) % 4, pyl, pc), wrecv.at[xrel, yl, c],
            ws.at[1 + (d * 2 + dy) * 2 + pc], wr.at[xrel, yl, c],
            dev(z, y if dy == 0 else yp, x + step, pc),
        )

    def w_cross(pc):
        return remote(
            w_src(x, 1 - yl, pc), wrecv.at[0, yl, c], ws.at[9 + pc], wr.at[0, yl, c],
            dev(z, yp, x, pc),
        )

    def w_forward(d, dy):
        step = 1 if d == 0 else -1
        return remote(
            wrelay.at[d, dy], wrecv.at[2, yl, c], fs.at[d, dy], wr.at[2, yl, c],
            dev(z, y if dy == 0 else yp, x + step, d),
        )

    for d in range(2):
        w_relay(d, 0).start()
    for pc in range(2):
        w_cross(pc).start()
    for d in range(2):
        for pc in range(2):
            w_direct(d, 0, pc).start()
    for d in range(2):
        w_relay(d, 1).start()
    for d in range(2):
        for pc in range(2):
            w_direct(d, 1, pc).start()

    got(tok_oth, tr)
    spread_r, spread_c = it(jnp.int32, (192, 384), 0), it(jnp.int32, (192, 384), 1)
    to_own = (spread_c == spread_r + c * 192).astype(F32).astype(BF)
    to_oth = (spread_c == spread_r + (1 - c) * 192).astype(F32).astype(BF)
    both = jnp.dot(tok_own[...], to_own, preferred_element_type=F32)
    both = both + jnp.dot(tok_oth[...], to_oth, preferred_element_type=F32)
    both = both.astype(BF)

    def place_of(o, js):
        oh, ol = (o % 8) // 2, o % 2
        return xbuf.at[
            js, c, 0, oh // 2,
            pl.ds(pl.multiple_of((oh % 2) * 48, 48), 48),
            pl.ds(pl.multiple_of(ol * 384, 384), 384),
        ]

    spot = it(jnp.int32, (CAP, 128), 0).astype(F32)
    for j in range(4):
        k = 2 * (3 - j) + c
        to = (z + 8 - k) % 8
        table = (slots[pl.ds(to, 1), :] == spot).astype(F32).astype(BF)
        placed[j] = jnp.dot(table, both, preferred_element_type=F32).astype(BF)
        if j < 3:
            remote(placed.at[j], place_of(y, j), zs.at[j], zr.at[j], dev(to, y, x, c)).start()
        else:
            @pl.when(c == 1)
            def _():
                remote(placed.at[j], place_of(y, j), zs.at[j], zr.at[j], dev(to, y, x, c)).start()

            @pl.when(c == 0)
            def _():
                pltpu.make_async_copy(placed.at[j], place_of(y, j), zl).start()

    def w_relayed(d, dy):
        got(wrelay.at[d, dy], rr.at[d, dy])
        w_forward(d, dy).start()

    def y_send(d, h, hf):
        o = y + 8 - (h - 1) if d == 0 else y + (h - 1)
        to = y + 1 if d == 0 else y + 7
        region = place_of(o, pl.ds(2 * hf, 2))
        return remote(region, region, ys.at[d, h - 1, hf], yr.at[d, h - 1, hf], dev(z, to, x, c))

    def y_got(d, h, hf):
        o = y + 8 - h if d == 0 else y + h
        got(place_of(o, pl.ds(2 * hf, 2)), yr.at[d, h - 1, hf])

    w_relayed(0, 0)
    w_relayed(1, 0)

    for hf in range(2):
        for j in (2 * hf, 2 * hf + 1):
            if j < 3:
                got(place_of(y, j), zr.at[j])
            else:
                @pl.when(c == 1)
                def _():
                    got(place_of(y, j), zr.at[j])

                @pl.when(c == 0)
                def _():
                    pltpu.make_async_copy(placed.at[j], place_of(y, j), zl).wait()
        y_send(0, 1, hf).start()
        y_send(1, 1, hf).start()
    for h in range(1, 4):
        for hf in range(2):
            for d in range(2):
                y_got(d, h, hf)
                if h < 3 or d == hf:
                    y_send(d, h + 1, hf).start()
        if h == 2:
            w_relayed(0, 1)
            w_relayed(1, 1)

    def unit(u):
        return u // 2, (u % 2 + yh // 2) % 2

    def x_own(u, d):
        j, hf = unit(u)
        return remote(
            xbuf.at[j, c, 0, hf], xbuf.at[j, c, 3 if d == 0 else 1, hf],
            xs.at[u, d], xr.at[u, d], dev(z, y, x + 1 if d == 0 else x + 3, c),
        )

    def x_half(u, d, xrel):
        j, hf = unit(u)
        return xbuf.at[j, c, xrel, hf, pl.ds(48 * d, 48)]

    def x_forward(u, d):
        return remote(
            x_half(u, d, 3 if d == 0 else 1), x_half(u, d, 2),
            xs.at[u, 2 + d], xr.at[u, 2 + d], dev(z, y, x + 1 if d == 0 else x + 3, c),
        )

    y_got(0, 4, 0)
    for u in range(2):
        x_own(u, 0).start()
        x_own(u, 1).start()
    y_got(1, 4, 1)

    two = 2 * rows
    pr, pc_ = it(jnp.int32, (two, two), 0), it(jnp.int32, (two, two), 1)
    apart = (pc_ == jnp.where(pr < rows, 2 * pr, 2 * (pr - rows) + 1)).astype(F32).astype(BF)

    def sort_piece(xrel, sl, sc):
        piece = wrecv[xrel, sl, sc].reshape(two, half)
        split = jnp.dot(apart, piece, preferred_element_type=F32).astype(BF)
        at = pl.ds(pl.multiple_of((sl * 2 + sc) * rows, rows), rows)
        wk[xrel, at, pl.ds(0, half)] = split[:rows]
        wk[xrel, at, pl.ds(half, half)] = split[rows:]

    own_w.wait()

    def take(i, carry):
        xrel, sl, sc = i // 4, (i // 2) % 2, i % 2
        mine = (xrel == 0) & (sl == yl) & (sc == c)

        @pl.when(jnp.logical_not(mine))
        def _():
            got(wrecv.at[xrel, sl, sc], wr.at[xrel, sl, sc])

        sort_piece(xrel, sl, sc)
        return carry

    lax.fori_loop(0, 16, take, 0)

    def swap(u):
        j, hf = unit(u)
        region = xbuf.at[j, c, :, hf]
        return remote(region, region, ds.at[u], dr.at[u], dev(z, y, x, 1 - c))

    def give(u, c2, q):
        j, hf = unit(u)
        k = 2 * (3 - j) + c2
        yhs = 2 * hf + q
        src = act.at[u, c2, pl.ds(48 * q, 48)]
        dst = ret.at[z, :, pl.ds(pl.multiple_of(yh * half, half), half)]
        mine = (k == 0) & (yhs == yh)
        return mine, src, dst, k, yhs

    def compute(u):
        j, hf = unit(u)
        acc = None
        for xrel in range(4):
            left = xbuf[j, :, xrel, hf].reshape(192, 768)
            part = jnp.dot(left, wk[xrel], preferred_element_type=F32)
            acc = part if acc is None else acc + part
        g, up = acc[:, :half], acc[:, half:]
        act[u] = (g / (1.0 + jnp.exp(-g)) * up).astype(BF).reshape(2, 96, half)
        for c2 in range(2):
            for q in range(2):
                mine, src, dst, k, yhs = give(u, c2, q)

                @pl.when(mine)
                def _():
                    pltpu.make_async_copy(src, dst, hl).start()

                @pl.when(jnp.logical_not(mine))
                def _():
                    remote(
                        src, dst, hs.at[k, yhs], hr.at[k, yh],
                        ((z + k) % 8 * 4 + yhs, b),
                    ).start()

    def turn(u, carry):
        @pl.when(u < 8)
        def _():
            for d in range(2):
                j, hf = unit(u)
                got(xbuf.at[j, c, 3 if d == 0 else 1, hf], xr.at[u, d])
                x_forward(u, d).start()

        @pl.when(u < 6)
        def _():
            for d in range(2):
                x_own(u + 2, d).start()

        @pl.when((u >= 1) & (u < 9))
        def _():
            for d in range(2):
                got(x_half(u - 1, d, 2), xr.at[u - 1, 2 + d])
            swap(u - 1).start()

        @pl.when(u >= 2)
        def _():
            j, hf = unit(u - 2)
            got(xbuf.at[j, 1 - c, :, hf], dr.at[u - 2])
            compute(u - 2)

        return carry

    lax.fori_loop(0, 10, turn, 0)

    ids = ids_ref[...]
    lane = it(jnp.int32, (128, 128), 1)
    row = it(jnp.int32, (128, 128), 0)
    names = ((ids[:, 0:1] == lane) | (ids[:, 1:2] == lane)).astype(F32)
    lower = (lane < row).astype(F32).astype(BF)
    ahead = jnp.dot(lower, names.astype(BF), preferred_element_type=F32)
    wide = it(jnp.int32, (128, E * CAP), 1).astype(F32)
    picks = []
    for kk in range(2):
        one = ids[:, kk : kk + 1]
        pos = jnp.sum(jnp.where(one == lane, ahead, 0.0), axis=1, keepdims=True)
        picks.append((wide == pos + one.astype(F32) * CAP).astype(F32).astype(BF))

    def back(i, carry):
        k, ys_ = i // 4, i % 4
        mine = (k == 0) & (ys_ == yh)
        src_z = (z + 8 - k) % 8
        dst = ret.at[src_z, :, pl.ds(pl.multiple_of(ys_ * half, half), half)]

        @pl.when(mine)
        def _():
            pltpu.make_async_copy(dst, dst, hl).wait()

        @pl.when(jnp.logical_not(mine))
        def _():
            got(dst, hr.at[k, ys_])
            sent(dst, hs.at[k, ys_])

        return carry

    lax.fori_loop(0, 32, back, 0)
    came = ret[...].reshape(E * CAP, 4 * half)
    for kk in range(2):
        out_ref[kk] = jnp.dot(picks[kk], came, preferred_element_type=F32).astype(BF)

    sent(tok_own, ts)
    piece = wrecv.at[0, 0, 0]
    for i in range(11):
        sent(piece, ws.at[i])
    for d in range(2):
        for dy in range(2):
            sent(piece, rs.at[d, dy])
            sent(piece, fs.at[d, dy])
    for j in range(3):
        sent(placed.at[j], zs.at[j])

    @pl.when(c == 1)
    def _():
        sent(placed.at[3], zs.at[3])

    for h in range(1, 5):
        for hf in range(2):
            for d in range(2):
                if h < 4 or d == hf:
                    sent(place_of(y, pl.ds(2 * hf, 2)), ys.at[d, h - 1, hf])

    def gone(u, carry):
        for d in range(2):
            sent(xbuf.at[0, c, 0, 0], xs.at[u, d])
            sent(x_half(0, d, 2), xs.at[u, 2 + d])
        sent(xbuf.at[0, c, :, 0], ds.at[u])
        return carry

    lax.fori_loop(0, 8, gone, 0)


def local(tokens, expert_ids, joined_weight):
    w = joined_weight[0]
    rows = w.shape[0]
    dma = pltpu.SemaphoreType.DMA
    vmem = pl.BlockSpec(memory_space=pltpu.VMEM)
    out = pl.pallas_call(
        kernel,
        out_shape=jax.ShapeDtypeStruct((2, 128, 1024), BF),
        in_specs=[vmem, vmem, vmem, pl.BlockSpec(memory_space=pltpu.HBM)],
        out_specs=vmem,
        scratch_shapes=[
            pltpu.VMEM((4, 2, 4, 2, 96, 768), BF),
            pltpu.VMEM((4, 2, 2, rows, 2, 256), BF),
            pltpu.VMEM((2, 2, rows, 2, 256), BF),
            pltpu.VMEM((4, 768, 512), BF),
            pltpu.VMEM((128, 192), BF),
            pltpu.VMEM((128, 192), BF),
            pltpu.VMEM((4, CAP, 384), BF),
            pltpu.VMEM((8, 128), F32),
            pltpu.VMEM((8, 2, 96, 256), BF),
            pltpu.VMEM((8, CAP, 1024), BF),
            dma((11,)), dma((4, 2, 2)), dma((2, 2)), dma((2, 2)), dma((2, 2)), dma,
            dma, dma, dma((4,)), dma((4,)), dma,
            dma((2, 4, 2)), dma((2, 4, 2)), dma((8, 4)), dma((8, 4)),
            dma((8,)), dma((8,)), dma((8, 4)), dma((8, 4)), dma,
        ],
        compiler_params=pltpu.CompilerParams(
            collective_id=0, has_side_effects=True, vmem_limit_bytes=60 * 1024 * 1024
        ),
    )(tokens, expert_ids, expert_ids.T, w)
    return out.reshape(2, 128, 4, 256).transpose(1, 0, 2, 3)


def solution(mesh):
    placed = (P("expert", "tensor"), P("expert", None), P("expert", "tensor", None, None))
    return jax.shard_map(
        local,
        mesh=mesh,
        in_specs=placed,
        out_specs=P("expert", None, None, "tensor"),
        check_vma=False,
    )
```

time: 301 us -> 122 us (0.41)
  the two profiles are of different devices: /device:TPU:10 before, /device:TPU:1 now
where the time goes in v1:
time: 122 us; the launch traced here: 121 us
  Pallas kernels  116 us (95%)
  local copies, waits for them, and re-layouts  5.35 us (4%)
    pallas_call x1, Pallas kernels, local(): pl.pallas_call(kernel, out_shape=jax.ShapeDtypeStruct((2, 128, 1024), BF)...  116 us
    unnamed x2, local copies, waits for them, and re-layouts  2.93 us

profile of v1, /device:TPU:1, one launch (start us, length us, event | category | flops | bytes accessed | tf_op | source)
XLA Modules:
  0.0 121.3 jit_solution(15391372430005521239)
XLA Ops:
  0.0 1.5 %copy.4.tok_ref = bf16[128,192]{1,0:T(8,128)(2,1)} copy(bf16[128,192]{0,1:T(8,128)(2,1)} %param.3) | data formatting | bytes 98304 | tf_op args[0]
  1.5 1.4 %copy.5.ids_ref = s32[128,2]{1,0:T(8,128)} copy(s32[128,2]{0,1:T(2,128)} %param.4) | data formatting | bytes 2048 | tf_op args[1]
  2.9 115.9 %shard_map.37 = bf16[2,128,1024]{2,1,0:T(8,128)(2,1)} custom-call(bf16[128,192]{1,0:T(8,128)(2,1)} %copy.4.tok_ref, s32[128,2]{1,0:T(8,128)} %copy.5.ids_ref, s32[2,128]{1,0:T(2,128)} %bitcast.6, bf16[192,2,4096]{2,1,0:T(2,128)(2,1)} %bitcast.5), custom_call_target="tpu_custom_call" | custom-call | tf_op jit(solution)/shard_map/pallas_call | solution.py:398
  118.9 1.4 %reshape.3 = bf16[2,128,4,256]{3,2,1,0:T(4,128)(2,1)S(1)} reshape(bf16[2,128,1024]{2,1,0:T(8,128)(2,1)} %shard_map.37) | data formatting | bytes 1048576 | tf_op jit(solution)/shard_map/reshape | solution.py:423
  120.3 1.0 copy.8

commit v2 on v0

v2 whole, which is shorter than its diff:
```python
import functools

import jax
import jax.numpy as jnp
from jax import lax
from jax.experimental import pallas as pl
from jax.experimental.pallas import tpu as pltpu
from jax.sharding import PartitionSpec as P

MESH = pl.DeviceIdType.MESH
E = 8
CAP = 48
BF = jnp.bfloat16
F32 = jnp.float32


def kernel(
    tok_ref, ids_ref, w_ref, out_ref,
    xbuf, wrecv, crelay, wk, tok, placed, slots, act, back_y, ret,
    ws, wsend, wr, cr, own_sem, ts, tr, zs, zr, zl,
    ys, yr, xs, xr, ns, nr, ds, dr, hs, hy, hyr, hr, hl,
):
    a, b = lax.axis_index("expert"), lax.axis_index("tensor")
    z, yh = a // 4, a % 4
    yl, x, c = b // 8, (b // 2) % 4, b % 2
    y = 2 * yh + yl

    def dev(zz, yy, xx, cc):
        yy, xx, zz = yy % 8, xx % 4, zz % 8
        return (zz * 4 + yy // 2, (yy % 2) * 8 + xx * 2 + cc)

    yp = y + 1 - 2 * yl
    rows = w_ref.shape[0]
    half = 256

    def remote(src, dst, send, recv, to):
        return pltpu.make_async_remote_copy(
            src_ref=src, dst_ref=dst, send_sem=send, recv_sem=recv,
            device_id=to, device_id_type=MESH,
        )

    me = dev(z, y, x, 1 - c)

    def got(ref, sem):
        remote(ref, ref, sem, sem, me).wait_recv()

    def sent(ref, sem):
        remote(ref, ref, sem, sem, me).wait_send()

    barrier = pltpu.get_barrier_semaphore()
    count = 0

    def greet(to):
        pl.semaphore_signal(barrier, inc=1, device_id=to, device_id_type=MESH)

    for dx in range(4):
        for dy in range(2):
            for dc in range(2):
                if dx or dy or dc:
                    greet(dev(z, y if dy == 0 else yp, x + dx, c if dc == 0 else 1 - c))
                    count += 1
    for k in range(1, 8):
        greet(dev(z + k, y, x, c))
        count += 1
    greet(dev(z, y - 1 + 2 * yl, x, c))
    count += 1

    tok[c] = tok_ref[...]
    it = lax.broadcasted_iota
    ids_t = ids_ref[...]
    named = (ids_t[0:1, :] == it(jnp.int32, (8, 128), 0)) | (ids_t[1:2, :] == it(jnp.int32, (8, 128), 0))
    before = (it(jnp.int32, (128, 128), 0) < it(jnp.int32, (128, 128), 1)).astype(F32).astype(BF)
    earlier = jnp.dot(named.astype(F32).astype(BF), before, preferred_element_type=F32)
    slots[...] = jnp.where(named, earlier, -1.0)

    pl.semaphore_wait(barrier, count)

    tok_copy = remote(tok.at[c], tok.at[c], ts, tr, dev(z, y, x, 1 - c))
    tok_copy.start()

    def w_src(px, py, pc):
        col = (py * 8 + px * 2 + pc) * half
        return w_ref.at[:, :, pl.ds(pl.multiple_of(col, half), half)]

    own_w = pltpu.make_async_copy(w_src(x, yl, c), wrecv.at[0, yl, c], own_sem)
    own_w.start()
    other_w = remote(w_src(x, yl, 1 - c), wrecv.at[0, yl, c], ws, wr.at[0, yl, c], dev(z, y, x, 1 - c))
    other_w.start()

    def along(d):
        return dev(z, y, x + 1 if d == 0 else x + 3, c)

    def w_direct(step, pc):
        return remote(
            w_src((x + step) % 4, yl, pc), wrecv.at[4 - step, yl, c],
            wsend, wr.at[4 - step, yl, c], dev(z, y, x + step, pc),
        )

    def w_cross(step, pc):
        src = w_src((x + step) % 4, 1 - yl, pc)
        if step == 0:
            return remote(src, wrecv.at[0, yl, c], wsend, wr.at[0, yl, c], dev(z, yp, x, pc))
        return remote(src, crelay.at[step - 1, pc], wsend, cr.at[step - 1, pc], dev(z, yp, x, c))

    def c_direct(step, pc):
        return remote(
            crelay.at[step - 1, pc], wrecv.at[4 - step, 1 - yl, c],
            wsend, wr.at[4 - step, 1 - yl, c], dev(z, y, x + step, pc),
        )

    for pc in range(2):
        w_direct(2, pc).start()
    for pc in range(2):
        w_cross(2, pc).start()
    for pc in range(2):
        for step in (1, 3):
            w_direct(step, pc).start()

    got(tok.at[1 - c], tr)
    both = tok[...].reshape(384, 128)

    def piece_of(o, xrel, start, size, cc):
        oh, ol = (o % 8) // 2, o % 2
        return xbuf.at[
            cc, xrel, oh, pl.ds(start, size), pl.ds(pl.multiple_of(ol * 384, 384), 384)
        ]

    spot = it(jnp.int32, (CAP, 128), 0).astype(F32)
    for j in range(4):
        k = (4, 6, 2, 0)[j] - c
        to = (z + 8 - k) % 8
        table = (slots[pl.ds(to, 1), :] == spot).astype(F32).astype(BF)
        placed[j] = lax.dot_general(
            table, both, (((1,), (1,)), ((), ())), preferred_element_type=F32
        ).astype(BF)
        if j < 3:
            remote(placed.at[j], piece_of(y, 0, 48 * j, 48, c), zs.at[j], zr.at[j], dev(to, y, x, c)).start()
        else:
            @pl.when(c == 1)
            def _():
                remote(placed.at[j], piece_of(y, 0, 48 * j, 48, c), zs.at[j], zr.at[j], dev(to, y, x, c)).start()

            @pl.when(c == 0)
            def _():
                pltpu.make_async_copy(placed.at[j], piece_of(y, 0, 48 * j, 48, c), zl).start()

    def y_send(d, h, hf):
        o = y + 8 - (h - 1) if d == 0 else y + (h - 1)
        to = y + 1 if d == 0 else y + 7
        region = piece_of(o, 0, 96 * hf, 96, c)
        return remote(region, region, ys.at[d, h - 1, hf], yr.at[d, h - 1, hf], dev(z, to, x, c))

    def y_got(d, h, hf):
        o = y + 8 - h if d == 0 else y + h
        got(piece_of(o, 0, 96 * hf, 96, c), yr.at[d, h - 1, hf])

    def y_round(h):
        for hf in range(2):
            for d in range(2):
                y_got(d, h, hf)
                if h < 3 or d == hf:
                    y_send(d, h + 1, hf).start()

    side = 2 * yl - 1

    def origin(v):
        away = (0, 0, -1, -1, -2, -3, 3, 4, 3, 4, -2, -3, 1, 1, 2, 2)[v]
        return (y + 8 + side * away) % 8

    def part(v, xrel, cc, start=0, size=96):
        o, near = origin(v), (0, 1, 0, 1, 0, 0, 0, 0, 1, 1, 1, 1, 0, 1, 0, 1)[v]
        return xbuf.at[
            cc, xrel, o // 2, pl.ds(96 * near + start, size),
            pl.ds(pl.multiple_of(o % 2 * 384, 384), 384),
        ]

    def x_own(v, d):
        return remote(
            part(v, 0, c), part(v, 3 if d == 0 else 1, c), xs, xr.at[v, d], along(d)
        )

    def x_forward(v, d):
        return remote(
            part(v, 3 if d == 0 else 1, c, 48 * d, 48), part(v, 2, c, 48 * d, 48),
            xs, xr.at[v, 2], along(d),
        )

    def x_start(u):
        for d in range(2):
            x_own(u, d).start()

    def c_directed(step, pc):
        got(crelay.at[step - 1, pc], cr.at[step - 1, pc])
        c_direct(step, pc).start()

    for hf in range(2):
        for j in (2 * hf, 2 * hf + 1):
            if j < 3:
                got(piece_of(y, 0, 48 * j, 48, c), zr.at[j])
            else:
                @pl.when(c == 1)
                def _():
                    got(piece_of(y, 0, 48 * j, 48, c), zr.at[j])

                @pl.when(c == 0)
                def _():
                    pltpu.make_async_copy(placed.at[j], piece_of(y, 0, 48 * j, 48, c), zl).wait()
        y_send(0, 1, hf).start()
        y_send(1, 1, hf).start()
    two = 2 * rows
    pr, pc_ = it(jnp.int32, (two, two), 0), it(jnp.int32, (two, two), 1)
    apart = (pc_ == jnp.where(pr < rows, 2 * pr, 2 * (pr - rows) + 1)).astype(F32).astype(BF)

    def sort_piece(xrel, sl, sc):
        piece = wrecv[xrel, sl, sc].reshape(two, half)
        split = jnp.dot(apart, piece, preferred_element_type=F32).astype(BF)
        at = pl.ds(pl.multiple_of((sl * 2 + sc) * rows, rows), rows)
        wk[xrel, at, pl.ds(0, half)] = split[:rows]
        wk[xrel, at, pl.ds(half, half)] = split[rows:]

    def take(row):
        def one(i, carry):
            xrel, sc = i // 2, i % 2
            mine = (xrel == 0) & (row == yl) & (sc == c)

            @pl.when(jnp.logical_not(mine))
            def _():
                got(wrecv.at[xrel, row, sc], wr.at[xrel, row, sc])

            sort_piece(xrel, row, sc)
            return carry

        lax.fori_loop(0, 8, one, 0)

    def swap(v):
        region = part(v, pl.ds(0, 4), c)
        return remote(region, region, ds, dr.at[v], dev(z, y, x, 1 - c))

    def gather(v):
        for d in range(2):
            got(part(v, 3 if d == 0 else 1, c), xr.at[v, d])
            x_forward(v, d).start()
        if v < 10:
            x_start(v + 2)

    def collect(v):
        got(part(v, 2, c), xr.at[v, 2])
        swap(v).start()
        if v < 4:
            region = part(v, pl.ds(1, 3), c)
            remote(region, region, ns, nr.at[v], dev(z, y + side + 8, x, c)).start()

    def collect_near(v):
        got(part(v, pl.ds(1, 3), c), nr.at[v - 12])
        swap(v).start()

    firsts, lasts = (0, 1, 12, 13, 4, 10, 6, 8), (2, 3, 14, 15, 5, 11, 7, 9)

    def hand(store, i, by, to):
        for c2 in range(2):
            for q in range(2):
                k = ((2 - 2 * q if i % 2 else 4 + 2 * q) - c2) % 8
                src = store.at[4 * i + 2 * c2 + q]
                dst = ret.at[z, :, pl.ds(pl.multiple_of(by * half, half), half)]
                if k == 0 and to is yh:
                    pltpu.make_async_copy(src, dst, hl.at[by]).start()
                else:
                    remote(src, dst, hs, hr.at[k, by], ((z + k) % 8 * 4 + to, b)).start()

    def giver(i):
        return (yh + 8 - (origin(lasts[i]) // 2 - yh)) % 4

    def pass_on(i):
        got(back_y.at[pl.ds(4 * i, 4)], hyr.at[i])
        hand(back_y, i, giver(i), yh)

    def finish(i):
        first, last, near = firsts[i], lasts[i], i % 2
        got(part(first, pl.ds(0, 4), 1 - c), dr.at[first])
        got(part(last, pl.ds(0, 4), 1 - c), dr.at[last])
        yhs = origin(last) // 2
        acc = None
        for xrel in range(4):
            left = xbuf[:, xrel, yhs, pl.ds(96 * near, 96), :].reshape(192, 768)
            term = jnp.dot(left, wk[xrel], preferred_element_type=F32)
            acc = term if acc is None else acc + term
        g, up = acc[:, :half], acc[:, half:]
        act[pl.ds(4 * i, 4)] = (g / (1.0 + jnp.exp(-g)) * up).astype(BF).reshape(4, CAP, half)
        if i < 2:
            hand(act, i, yh, yh)
        elif i == 5:
            hand(act, i, yh, yhs)
        else:
            mine = act.at[pl.ds(4 * i, 4)]
            remote(mine, back_y.at[pl.ds(4 * i, 4)], hy, hyr.at[i], (z * 4 + yhs, b)).start()

    x_start(0)
    x_start(1)
    w_cross(1, 0).start()
    for pc in range(2):
        c_directed(2, pc)
    y_round(1)
    w_cross(3, 0).start()
    y_round(2)
    w_cross(1, 1).start()
    c_directed(1, 0)
    gather(0)
    gather(1)
    y_round(3)
    w_cross(3, 1).start()
    for pc in range(2):
        w_cross(0, pc).start()
    c_directed(3, 0)
    c_directed(1, 1)
    gather(2)
    collect(0)
    collect(1)
    own_w.wait()
    take(yl)
    c_directed(3, 1)
    gather(3)
    gather(4)
    y_got(0, 4, 0)
    y_got(1, 4, 1)
    collect(2)
    collect(3)
    gather(5)
    take(1 - yl)
    collect_near(12)
    collect_near(13)
    finish(0)
    gather(6)
    finish(1)
    collect(4)
    collect(5)
    gather(7)
    finish(4)
    gather(8)
    collect(6)
    collect_near(14)
    collect(7)
    finish(6)
    gather(9)
    collect_near(15)
    finish(2)
    pass_on(4)
    gather(10)
    collect(8)
    finish(3)
    collect(9)
    gather(11)
    pass_on(2)
    finish(7)
    collect(10)
    pass_on(6)
    pass_on(3)
    collect(11)
    finish(5)
    pass_on(7)

    chosen = None
    for kk in range(2):
        one = ids_t[kk : kk + 1, :]
        pos = jnp.sum(jnp.where(one == it(jnp.int32, (8, 128), 0), earlier, 0.0), axis=0, keepdims=True)
        spread = (it(jnp.int32, (128, 256), 1) == 2 * it(jnp.int32, (128, 256), 0) + kk).astype(F32).astype(BF)
        pair = jnp.concatenate([one.astype(F32), pos, jnp.zeros((6, 128), F32)], axis=0).astype(BF)
        part = jnp.dot(pair, spread, preferred_element_type=F32)
        chosen = part if chosen is None else chosen + part
    took = chosen[0:1, :] * CAP + chosen[1:2, :]
    pick = (it(jnp.int32, (E * CAP, 256), 0).astype(F32) == took).astype(F32).astype(BF)

    def back(i, carry):
        k, by = i // 4, i % 4
        dst = ret.at[(z + 8 - k) % 8, :, pl.ds(pl.multiple_of(by * half, half), half)]

        stays = (k == 0) & (by != giver(5))

        @pl.when(stays)
        def _():
            pltpu.make_async_copy(dst, dst, hl.at[by]).wait()

        @pl.when(jnp.logical_not(stays))
        def _():
            got(dst, hr.at[k, by])

        return carry

    lax.fori_loop(0, 32, back, 0)
    came = ret[...].reshape(E * CAP, 4 * half)
    out_ref[...] = lax.dot_general(
        pick, came, (((0,), (0,)), ((), ())), preferred_element_type=F32
    ).astype(BF)

    sent(tok.at[c], ts)
    sent(wrecv.at[0, 0, 0], ws)
    sent(xbuf.at[c, :, :, pl.ds(0, 160)], wsend)
    sent(xbuf.at[c, pl.ds(0, 3), pl.ds(0, 3)], xs)
    sent(xbuf.at[c, 0, pl.ds(0, 3)], ns)
    sent(xbuf.at[c], ds)
    sent(act.at[pl.ds(0, 29)], hs)
    sent(act.at[pl.ds(0, 20)], hy)
    for j in range(3):
        sent(placed.at[j], zs.at[j])

    @pl.when(c == 1)
    def _():
        sent(placed.at[3], zs.at[3])

    for h in range(1, 5):
        for hf in range(2):
            for d in range(2):
                if h < 4 or d == hf:
                    sent(piece_of(y, 0, 96 * hf, 96, c), ys.at[d, h - 1, hf])


def local(tokens, expert_ids, joined_weight):
    w = joined_weight[0]
    rows = w.shape[0]
    dma = pltpu.SemaphoreType.DMA
    vmem = pl.BlockSpec(memory_space=pltpu.VMEM)
    out = pl.pallas_call(
        kernel,
        out_shape=jax.ShapeDtypeStruct((256, 1024), BF),
        in_specs=[vmem, vmem, pl.BlockSpec(memory_space=pltpu.HBM)],
        out_specs=vmem,
        scratch_shapes=[
            pltpu.VMEM((2, 4, 4, 192, 768), BF),
            pltpu.VMEM((4, 2, 2, rows, 2, 256), BF),
            pltpu.VMEM((3, 2, rows, 2, 256), BF),
            pltpu.VMEM((4, 768, 512), BF),
            pltpu.VMEM((2, 192, 128), BF),
            pltpu.VMEM((4, CAP, 384), BF),
            pltpu.VMEM((8, 128), F32),
            pltpu.VMEM((32, CAP, 256), BF),
            pltpu.VMEM((32, CAP, 256), BF),
            pltpu.VMEM((8, CAP, 1024), BF),
            dma, dma, dma((4, 2, 2)), dma((3, 2)), dma,
            dma, dma, dma((4,)), dma((4,)), dma,
            dma((2, 4, 2)), dma((2, 4, 2)), dma, dma((12, 3)), dma, dma((4,)),
            dma, dma((16,)), dma, dma, dma((8,)), dma((8, 4)), dma((4,)),
        ],
        compiler_params=pltpu.CompilerParams(
            collective_id=0, has_side_effects=True, vmem_limit_bytes=60 * 1024 * 1024
        ),
    )(tokens.T, expert_ids.T, w)
    return out.reshape(128, 2, 4, 256)


def solution(mesh):
    placed = (P("expert", "tensor"), P("expert", None), P("expert", "tensor", None, None))
    return jax.shard_map(
        local,
        mesh=mesh,
        in_specs=placed,
        out_specs=P("expert", None, None, "tensor"),
        check_vma=False,
    )
```

time: 301 us -> 103 us (0.34)
  the two profiles are of different devices: /device:TPU:10 before, /device:TPU:1 now
where the time goes in v2:
time: 103 us; the launch traced here: 102 us
  Pallas kernels  100 us (97%)
  local copies, waits for them, and re-layouts  2.23 us (2%)
    pallas_call x1, Pallas kernels, local(): pl.pallas_call(kernel, out_shape=jax.ShapeDtypeStruct((256, 1024), BF), i...  100 us
    reshape x1, local copies, waits for them, and re-layouts, local(): return out.reshape(128, 2, 4, 256)  2.23 us

profile of v2, /device:TPU:1, one launch (start us, length us, event | category | flops | bytes accessed | tf_op | source)
XLA Modules:
  0.0 102.3 jit_solution(6577517568134544470)
XLA Ops:
  0.0 100.1 %shard_map.37 = bf16[256,1024]{1,0:T(8,128)(2,1)} custom-call(bf16[192,128]{1,0:T(8,128)(2,1)} %bitcast.4, s32[2,128]{1,0:T(2,128)} %bitcast.5, bf16[192,2,4096]{2,1,0:T(2,128)(2,1)} %bitcast.3), custom_call_target="tpu_custom_call" | custom-call | tf_op jit(solution)/shard_map/pallas_call | solution.py:421
  100.1 2.2 %reshape.3 = bf16[128,2,4,256]{3,2,1,0:T(4,128)(2,1)} reshape(bf16[256,1024]{1,0:T(8,128)(2,1)} %shard_map.37) | data formatting | bytes 1048576 | tf_op jit(solution)/shard_map/reshape | solution.py:446

commit v3 on v2

--- a/solution.py
+++ b/solution.py
@@ -16,7 +16,7 @@
 
 def kernel(
     tok_ref, ids_ref, w_ref, out_ref,
-    xbuf, wrecv, crelay, wk, tok, placed, slots, act, back_y, ret,
+    xbuf, wrecv, crelay, wk, tok, placed, slots, act, back_y, ret, rows_out, packed,
     ws, wsend, wr, cr, own_sem, ts, tr, zs, zr, zl,
     ys, yr, xs, xr, ns, nr, ds, dr, hs, hy, hyr, hr, hl,
 ):
@@ -112,9 +112,8 @@
         w_direct(2, pc).start()
     for pc in range(2):
         w_cross(2, pc).start()
-    for pc in range(2):
-        for step in (1, 3):
-            w_direct(step, pc).start()
+    for step in (1, 3):
+        w_direct(step, 0).start()
 
     got(tok.at[1 - c], tr)
     both = tok[...].reshape(384, 128)
@@ -240,8 +239,8 @@
         for d in range(2):
             got(part(v, 3 if d == 0 else 1, c), xr.at[v, d])
             x_forward(v, d).start()
-        if v < 10:
-            x_start(v + 2)
+        for later in ((), (), (), (), (6,), (7, 8), (9,), (10,), (11,), (), (), ())[v]:
+            x_start(later)
 
     def collect(v):
         got(part(v, 2, c), xr.at[v, 2])
@@ -288,7 +287,7 @@
         act[pl.ds(4 * i, 4)] = (g / (1.0 + jnp.exp(-g)) * up).astype(BF).reshape(4, CAP, half)
         if i < 2:
             hand(act, i, yh, yh)
-        elif i == 5:
+        elif i in (5, 7):
             hand(act, i, yh, yhs)
         else:
             mine = act.at[pl.ds(4 * i, 4)]
@@ -296,67 +295,72 @@
 
     x_start(0)
     x_start(1)
+    for step in (1, 3):
+        w_direct(step, 1).start()
     w_cross(1, 0).start()
-    for pc in range(2):
-        c_directed(2, pc)
     y_round(1)
     w_cross(3, 0).start()
+    x_start(2)
+    x_start(3)
+    gather(0)
+    gather(1)
+    c_directed(2, 0)
     y_round(2)
     w_cross(1, 1).start()
+    gather(2)
+    gather(3)
+    c_directed(2, 1)
     c_directed(1, 0)
-    gather(0)
-    gather(1)
+    c_directed(3, 0)
+    collect(0)
     y_round(3)
     w_cross(3, 1).start()
     for pc in range(2):
         w_cross(0, pc).start()
-    c_directed(3, 0)
+    x_start(4)
+    x_start(5)
+    collect(1)
+    collect(2)
     c_directed(1, 1)
-    gather(2)
-    collect(0)
-    collect(1)
+    collect(3)
     own_w.wait()
     take(yl)
     c_directed(3, 1)
-    gather(3)
-    gather(4)
     y_got(0, 4, 0)
     y_got(1, 4, 1)
-    collect(2)
-    collect(3)
+    collect_near(12)
+    gather(4)
     gather(5)
+    collect_near(13)
     take(1 - yl)
-    collect_near(12)
-    collect_near(13)
-    finish(0)
     gather(6)
-    finish(1)
+    collect_near(14)
     collect(4)
     collect(5)
+    finish(0)
+    finish(2)
     gather(7)
     finish(4)
+    collect_near(15)
+    finish(1)
+    collect(6)
     gather(8)
-    collect(6)
-    collect_near(14)
+    finish(3)
     collect(7)
+    gather(9)
     finish(6)
-    gather(9)
-    collect_near(15)
-    finish(2)
-    pass_on(4)
+    collect(8)
     gather(10)
-    collect(8)
-    finish(3)
+    pass_on(2)
     collect(9)
     gather(11)
-    pass_on(2)
+    pass_on(4)
     finish(7)
     collect(10)
-    pass_on(6)
-    pass_on(3)
     collect(11)
     finish(5)
-    pass_on(7)
+    pass_on(3)
+    pass_on(6)
 
     chosen = None
     for kk in range(2):
@@ -373,7 +377,7 @@
         k, by = i // 4, i % 4
         dst = ret.at[(z + 8 - k) % 8, :, pl.ds(pl.multiple_of(by * half, half), half)]
 
-        stays = (k == 0) & (by != giver(5))
+        stays = (k == 0) & (by != giver(5)) & (by != giver(7))
 
         @pl.when(stays)
         def _():
@@ -387,9 +391,16 @@
 
     lax.fori_loop(0, 32, back, 0)
     came = ret[...].reshape(E * CAP, 4 * half)
-    out_ref[...] = lax.dot_general(
+    total = lax.dot_general(
         pick, came, (((0,), (0,)), ((), ())), preferred_element_type=F32
-    ).astype(BF)
+    )
+    for r in range(4):
+        for h in range(2):
+            at = (2 * r + h) * 128
+            rows_out[pl.ds(4 * h + r, 256, stride=8), :] = total[:, at : at + 128]
+    packed[...] = rows_out[...].astype(BF)
+    leave = pltpu.make_async_copy(packed, out_ref, own_sem)
+    leave.start()
 
     sent(tok.at[c], ts)
     sent(wrecv.at[0, 0, 0], ws)
@@ -397,8 +408,8 @@
     sent(xbuf.at[c, pl.ds(0, 3), pl.ds(0, 3)], xs)
     sent(xbuf.at[c, 0, pl.ds(0, 3)], ns)
     sent(xbuf.at[c], ds)
-    sent(act.at[pl.ds(0, 29)], hs)
-    sent(act.at[pl.ds(0, 20)], hy)
+    sent(act.at[pl.ds(0, 30)], hs)
+    sent(act.at[pl.ds(0, 16)], hy)
     for j in range(3):
         sent(placed.at[j], zs.at[j])
 
@@ -411,6 +422,7 @@
             for d in range(2):
                 if h < 4 or d == hf:
                     sent(piece_of(y, 0, 96 * hf, 96, c), ys.at[d, h - 1, hf])
+    leave.wait()
 
 
 def local(tokens, expert_ids, joined_weight):
@@ -420,9 +432,9 @@
     vmem = pl.BlockSpec(memory_space=pltpu.VMEM)
     out = pl.pallas_call(
         kernel,
-        out_shape=jax.ShapeDtypeStruct((256, 1024), BF),
+        out_shape=jax.ShapeDtypeStruct((2048, 128), BF),
         in_specs=[vmem, vmem, pl.BlockSpec(memory_space=pltpu.HBM)],
-        out_specs=vmem,
+        out_specs=pl.BlockSpec(memory_space=pl.ANY),
         scratch_shapes=[
             pltpu.VMEM((2, 4, 4, 192, 768), BF),
             pltpu.VMEM((4, 2, 2, rows, 2, 256), BF),
@@ -434,16 +446,18 @@
             pltpu.VMEM((32, CAP, 256), BF),
             pltpu.VMEM((32, CAP, 256), BF),
             pltpu.VMEM((8, CAP, 1024), BF),
+            pltpu.VMEM((2048, 128), F32),
+            pltpu.VMEM((2048, 128), BF),
             dma, dma, dma((4, 2, 2)), dma((3, 2)), dma,
             dma, dma, dma((4,)), dma((4,)), dma,
             dma((2, 4, 2)), dma((2, 4, 2)), dma, dma((12, 3)), dma, dma((4,)),
             dma, dma((16,)), dma, dma, dma((8,)), dma((8, 4)), dma((4,)),
         ],
         compiler_params=pltpu.CompilerParams(
-            collective_id=0, has_side_effects=True, vmem_limit_bytes=60 * 1024 * 1024
+            collective_id=0, has_side_effects=True, vmem_limit_bytes=54000000
         ),
     )(tokens.T, expert_ids.T, w)
-    return out.reshape(128, 2, 4, 256)
+    return out.reshape(128, 2, 2, 4, 128).transpose(0, 1, 3, 2, 4).reshape(128, 2, 4, 256)
 
 
 def solution(mesh):

time: 103 us -> 96.5 us (0.937)
  Pallas kernels: 100 us -> 94.1 us
    pallas_call x1, Pallas kernels: 100 us -> 94.1 us  [local(): pl.pallas_call(kernel, out_shape=jax.ShapeDtypeStruct((2048, 128), BF), i...]
    unnamed x0 -> x5, local copies, waits for them, and re-layouts: none -> 2.27 us
    reshape x1 -> x0, local copies, waits for them, and re-layouts: 2.23 us -> none  [local(): return out.reshape(128, 2, 4, 256)]
where the time goes in v3:
time: 96.5 us; the launch traced here: 96.3 us
  Pallas kernels  94.1 us (98%)
  local copies, waits for them, and re-layouts  2.27 us (2%)
    pallas_call x1, Pallas kernels, local(): pl.pallas_call(kernel, out_shape=jax.ShapeDtypeStruct((2048, 128), BF), i...  94.1 us
    unnamed x5, local copies, waits for them, and re-layouts  2.27 us

profile of v3, /device:TPU:1, one launch (start us, length us, event | category | flops | bytes accessed | tf_op | source)
XLA Modules:
  0.0 96.3 jit_solution(42894483848971244)
XLA Ops:
  0.0 0.0 copy-start
  0.0 0.8 copy-done
  0.8 0.0 copy-start.1
  0.8 0.7 copy-done.1
  1.5 94.1 %shard_map.37 = bf16[2048,128]{1,0:T(8,128)(2,1)S(1)} custom-call(bf16[192,128]{1,0:T(8,128)(2,1)S(1)} %bitcast.9, s32[2,128]{1,0:T(2,128)S(1)} %bitcast.10, bf16[192,2,4096]{2,1,0:T(2,128)(2,1)} %bitcast.11), custom_call_target="tpu_custom_call" | custom-call | tf_op jit(solution)/shard_map/pallas_call | solution.py:433
  95.5 0.8 copy.6
Async XLA Ops:
  0.0 0.8 copy-start
  0.8 0.7 copy-start.1
